TPU v7x, 32 devices: a whole 2x2x4 slice. The times are simulated.
32 devices in a mesh: tm: 16 (over z, y, x), rep: 2 (over core).
Axes of the slice: x: 2, y: 2, z: 4, core: 2. Of those that a mesh axis runs over, the one named last changes fastest.
Arguments:
- rows: float32 [65536, 256], P('tm', 'rep'), may hold values from -90 to 90, as said below
- row_mask: int32 [65536], P('tm'), may hold values from 0 to 1, as said below
- key_bucket: int32 [65536], P('tm'), may hold values from 0 to 15
- gain: float32 [256], P('rep'), may hold values from 0.1 to 1.9
Outputs:
- keyed: float32 [49152, 256], P('tm', 'rep')
Inputs may be any that keep to these rules, and one draw needn't show every extreme that they name: `rows`: scale per column differs; entries stay in the range. `row_mask`: of the 4096 rows of each index of tm, at least 2048 pass. Among the passing rows of one index of tm, no key bucket occurs more than 192 times, and one bucket, the same for all indices, occurs exactly 192 times on every index.
All inputs are finite; a program needn't handle non-finite values.
Results may differ from a plain program's by a relative error of at most 0.0003.
Values sent between devices are 32-bit elements; how exact they have to be, the bound alone decides.
A program may use at most 64 MiB of HBM per device.

v0:
```python
import jax
import jax.numpy as jnp
from jax import lax
from jax.sharding import PartitionSpec as P

F = 256
WINDOW = 512
epsilon = 1e-06


def passed_along(x, axis, by):
    devices = lax.axis_size(axis)
    return lax.ppermute(x, axis, [(i, (i + by) % devices) for i in range(devices)])


def window_sums(extended, width):
    blocks = extended.reshape(-1, width, extended.shape[1])
    steps = jnp.arange(width, dtype=jnp.int32)
    lower = (steps[:, None] >= steps[None, :]).astype(jnp.float32)
    inner = jnp.einsum("ij,bjf->bif", lower, blocks, precision=lax.Precision.HIGHEST)
    totals = inner[:, -1:, :]
    result = inner[1:] + totals[:-1] - inner[:-1]
    return result.reshape(-1, extended.shape[1])


def bucket_ranks(hits):
    size_rows, buckets = hits.shape
    block = min(512, size_rows)
    grouped = hits.reshape(size_rows // block, block, buckets)
    steps = jnp.arange(block, dtype=jnp.int32)
    lower = (steps[:, None] >= steps[None, :]).astype(jnp.float32)
    within = jnp.einsum("ij,bjc->bic", lower, grouped, precision=lax.Precision.HIGHEST)
    totals = within[:, -1, :]
    earlier = jnp.cumsum(totals, axis=0) - totals
    running = (within + earlier[:, None, :]).reshape(size_rows, buckets)
    local_rank = (jnp.sum(running * hits, axis=1) - 1.0).astype(jnp.int32)
    counts = jnp.sum(totals, axis=0).astype(jnp.int32)
    return (local_rank, counts)


def compact_rows(payload, row_mask):
    size_rows, width = payload.shape
    live = row_mask == 1
    order_rank = jnp.cumsum(row_mask) - 1
    target = jnp.where(live, order_rank, size_rows)
    return jnp.zeros((size_rows, width), jnp.float32).at[target].set(payload, mode="drop")


def fill_slots(values, slot, slots_total):
    width = values.shape[1]
    return jnp.zeros((slots_total, width), jnp.float32).at[slot].set(values, mode="drop")


def local(rows, row_mask, key_bucket, gain):
    size_rows, half = rows.shape
    nodes = lax.axis_size("tm")
    most = 3 * size_rows // (4 * nodes)
    positions = jnp.arange(size_rows, dtype=jnp.int32)
    bucket_ids = jnp.arange(nodes, dtype=jnp.int32)
    count = jnp.sum(row_mask)
    own_hits = (key_bucket[:, None] == bucket_ids[None, :]).astype(jnp.float32)
    payload = jnp.concatenate([rows, own_hits], axis=1)
    packed = compact_rows(payload, row_mask)
    compact = packed[:, :half]
    hits = packed[:, half:]
    valid = positions < count
    key_value = jnp.dot(
        hits,
        bucket_ids.astype(jnp.float32),
        precision=lax.Precision.HIGHEST,
        preferred_element_type=jnp.float32,
    )
    compact_key = jnp.where(valid, key_value.astype(jnp.int32), nodes)
    tail = lax.dynamic_slice_in_dim(compact, count - WINDOW, WINDOW, 0)
    earlier_tail = passed_along(tail, "tm", 1)
    extended = jnp.concatenate([earlier_tail, compact], axis=0)
    sums = window_sums(extended, WINDOW)
    squares = jnp.sum(sums * sums, axis=1)
    full = lax.psum(squares, "rep")
    values = sums * gain[None, :] / jnp.sqrt(full[:, None] / F + epsilon)
    local_rank, counts = bucket_ranks(hits)
    slot = jnp.where(valid, compact_key * most + local_rank, nodes * most)
    outgoing = fill_slots(values, slot, nodes * most)
    outgoing = outgoing.reshape(nodes, most * half)
    sideband = counts.astype(jnp.float32)[:, None]
    received, got_side = (
        lax.all_to_all(outgoing, "tm", split_axis=0, concat_axis=0, tiled=True),
        lax.all_to_all(sideband, "tm", split_axis=0, concat_axis=0, tiled=True),
    )
    got_numbers = got_side.astype(jnp.int32)
    got_starts = jnp.cumsum(got_numbers, axis=0) - got_numbers
    capacity = nodes * most
    start_list = got_starts.reshape(-1)
    spots = jnp.arange(capacity, dtype=jnp.int32)
    sender = jnp.sum((start_list[None, :] <= spots[:, None]).astype(jnp.int32), axis=1) - 1
    sender = jnp.maximum(sender, 0)
    offset = spots - start_list[sender]
    inside = (offset >= 0) & (offset < most)
    lookup = sender * most + jnp.clip(offset, 0, most - 1)
    flat = received.reshape(-1, half)
    keyed = jnp.where(inside[:, None], flat[lookup], jnp.float32(0.0))
    return keyed


def solution(mesh):
    in_specs = (P("tm", "rep"), P("tm"), P("tm"), P("rep"))
    out_specs = P("tm", "rep")
    return jax.shard_map(local, mesh=mesh, in_specs=in_specs, out_specs=out_specs, check_vma=False)
```

profile of v0, /device:TPU:12, one launch (start us, length us, event | category | flops | bytes accessed | tf_op | source)
XLA Modules:
  0.0 128.5 jit_solution(7532041285759532426)
XLA Ops:
  0.0 1.0 reduce-window.14
  1.0 0.1 slice.54
  1.1 0.1 reduce-window.18
  1.1 0.1 slice_reduce_fusion.2
  1.2 1.4 %fusion.20 = (s32[]{:T(128)}, s32[4096]{0:T(1024)S(1)}) fusion(s32[4096]{0:T(1024)} %param.5, s32[32,128]{1,0:T(8,128)S(1)} %reduce-window.14, s32[32]{0:T(128)S(1)} %slice_reduce_fusion.2), kind=kLoop, calls=%fused_computation.53 | loop fusion | flops 32767 | bytes 49284 | tf_op jit(solution)/shard_map/reduce_sum | solution.py:60
  2.7 1.3 %fusion.7 = f32[4096,16]{1,0:T(8,128)S(1)} fusion(s32[4096]{0:T(1024)} %param.6), kind=kLoop, calls=%fused_computation.17 | loop fusion | flops 131072 | bytes 278528 | tf_op jit(solution)/shard_map/convert_element_type | solution.py:61
  4.0 20.2 %scatter_custom_fusion = f32[4096,144]{1,0:T(8,128)} fusion(s32[4096]{0:T(1024)S(1)} %get-tuple-element.10, f32[4096,16]{1,0:T(8,128)S(1)} %fusion.7, f32[]{:T(128)} %constant.74, f32[4096,128]{1,0:T(8,128)} %param.4, f32[]{:T(128)} %constant.14.clone.1), kind=kCustom, calls=%fused_computation.3 | custom fusion | flops 589824 | bytes 6553608 | tf_op jit(solution)/shard_map/scatter | solution.py:46
  24.2 1.7 %slice.58 = f32[4096,128]{1,0:T(8,128)S(1)} slice(f32[4096,144]{1,0:T(8,128)} %scatter_custom_fusion), slice={[0:4096], [0:128]} | slice | bytes 4194304 | tf_op jit(solution)/shard_map/slice | solution.py:64
  25.9 0.0 copy-start
  27.3 0.0 copy-done
  27.3 0.0 slice-start
  27.3 1.5 %collective-permute-start = (f32[512,128]{1,0:T(8,128)S(1)}, f32[512,128]{1,0:T(8,128)S(1)}, u32[]{:S(2)}, u32[]{:S(2)}) collective-permute-start(f32[512,128]{1,0:T(8,128)S(1)} %constant_dynamic-slice_fusion), channel_id=1, source_target_pairs={{0,2},{2,4},{4,6},{6,8},{8,10},{10,12},{12,14},{14,16},{16,18},{18... | collective-permute-start | bytes 786440 | tf_op jit(solution)/shard_map/ppermute | solution.py:13
  28.9 0.0 slice-done
  28.9 3.4 %convolution_bitcast_fusion.1 = f32[8,512,16]{1,2,0:T(8,128)S(1)} fusion(f32[8,512,16]{2,1,0:T(8,128)S(1)} %bitcast.56), kind=kOutput, calls=%fused_computation.19 | convolution fusion | flops 402915328 | bytes 524288 | tf_op jit(solution)/shard_map/ij,bjc->bic/dot_general | solution.py:32
  32.3 0.2 slice_reduce_fusion.1
  32.5 0.7 copy.33
  33.2 7.2 %all-to-all-start = ((f32[16,1,1]{2,1,0:T(1,128)}), f32[16,1,1]{2,1,0:T(1,128)S(1)}, u32[]{:S(2)}, u32[]{:S(2)}) async-start(f32[16,1,1]{2,1,0:T(1,128)} %copy.33), calls=%async_computation | async-start | bytes 16384 | tf_op jit(solution)/shard_map/all_to_all | solution.py:88
  40.4 0.2 fusion.22
  40.5 3.5 %fusion.15 = f32[1,4096]{1,0:T(1,128)S(1)} fusion(f32[4096,144]{1,0:T(8,128)} %scatter_custom_fusion), kind=kOutput, calls=%fused_computation.45 | convolution fusion | flops 786448 | bytes 2113536 | tf_op jit(solution)/shard_map/dot_general | solution.py:67
  44.0 0.1 broadcast_add_fusion
  44.1 0.6 copy.43
  44.8 0.0 copy-start.1
  44.8 2.6 %fusion.5 = f32[4096]{0:T(1024)S(1)} fusion(f32[8,512,16]{2,1,0:T(8,128)S(1)} %copy.43, f32[4096,144]{1,0:T(8,128)} %scatter_custom_fusion), kind=kLoop, calls=%fused_computation.13 | loop fusion | flops 126976 | bytes 540672 | tf_op jit(solution)/shard_map/reduce_sum | solution.py:36
  47.3 0.7 compare_select_fusion.1
  48.0 0.0 collective-permute-done
  48.0 0.0 copy-done.1
  48.0 0.2 pad_maximum_fusion
  48.2 3.9 %convolution_bitcast_fusion = f32[9,512,128]{1,2,0:T(8,128)S(1)} fusion(f32[9,512,128]{2,1,0:T(8,128)S(1)} %bitcast.57), kind=kOutput, calls=%fused_computation.18 | convolution fusion | flops 3624140800 | bytes 4718592 | tf_op jit(solution)/shard_map/ij,bjf->bif/dot_general | solution.py:20
  52.1 0.4 slice_reduce_fusion
  52.5 1.8 %multiply_reduce_fusion = (f32[8,512]{1,0:T(8,128)S(1)}, f32[8,512,128]{1,2,0:T(8,128)}) fusion(f32[9,512,128]{1,2,0:T(8,128)S(1)} %convolution_bitcast_fusion, f32[8,128]{1,0:T(8,128)S(1)} %slice_reduce_fusion), kind=kLoop, calls=%fused_computation.14 | loop fusion | flops 2093056 | bytes 6311936 | tf_op jit(solution)/shard_map/reduce_sum | solution.py:78
  54.2 0.0 copy-start.2
  54.2 1.9 %copy.38 = f32[8,512,128]{2,1,0:T(8,128)S(1)} copy(f32[8,512,128]{1,2,0:T(8,128)} %get-tuple-element.8) | data formatting | bytes 4194304 | tf_op jit(solution)/shard_map/sub | solution.py:22
  56.2 3.4 %psum.7 = f32[4096]{0:T(1024)S(1)} all-reduce(f32[4096]{0:T(1024)S(1)} %bitcast.61), channel_id=1, replica_groups=mesh['tm'=16,'rep'=2] {'rep'}, use_global_device_ids=true, to_apply=%region_10.11 | all-reduce | flops 4096 | bytes 32768 | tf_op jit(solution)/shard_map/psum | solution.py:79
  59.6 0.0 copy-done.2
  59.6 1.9 %fusion.4 = f32[4096,128]{1,0:T(8,128)} fusion(f32[8,512,128]{2,1,0:T(8,128)S(1)} %copy.38, f32[4096]{0:T(1024)S(1)} %add_sqrt_fusion, f32[128]{0:T(128)S(1)} %copy-done.2), kind=kLoop, calls=%fused_computation.11 | loop fusion | flops 1048576 | bytes 4211200 | tf_op jit(solution)/shard_map/div | solution.py:80
  61.5 12.1 %scatter_custom_fusion.1 = f32[3072,128]{1,0:T(8,128)} fusion(s32[4096]{0:T(1024)S(1)} %compare_select_fusion.1, f32[4096,128]{1,0:T(8,128)} %fusion.4, f32[]{:T(128)} %constant.14.clone.1), kind=kCustom, calls=%fused_computation.24 | custom fusion | bytes 1573376 | tf_op jit(solution)/shard_map/scatter | solution.py:51
  73.6 0.0 all-to-all-done
  73.6 6.9 %all-to-all-start.1 = ((f32[16,1,24576]{2,1,0:T(1,128)}), f32[16,1,24576]{2,1,0:T(1,128)S(1)}, u32[]{:S(2)}, u32[]{:S(2)}) async-start(f32[16,1,24576]{2,1,0:T(1,128)} %bitcast.29), calls=%async_computation.1 | async-start | bytes 3145728 | tf_op jit(solution)/shard_map/all_to_all | solution.py:87
  80.6 0.1 reduce.3
  80.7 0.4 convert_reduce_fusion.1
  81.1 0.7 fusion.21
  81.8 0.1 convert_reduce_fusion
  81.9 9.9 %compare_and_fusion = (pred[3072]{0:T(1024)(128)(4,1)S(1)}, s32[3072]{0:T(1024)S(1)}) fusion(s32[]{:T(128)} %bitcast.22, s32[]{:T(128)} %bitcast.21, s32[]{:T(128)} %bitcast.20, s32[]{:T(128)} %bitcast.19, s32[]{:T(128)} %bitcast.18, s32[]{:T(128)} %bitcast.17, s32[]{:T(128)} %bitcast.16, s32[]{:T(128)} %bitcast.15, s32[]{:T(128)} %bitcast.14, s32[]{:T(128)} %bitcast.13, ...), kind=kLoop, calls=%fused_computation.42 | loop fusion | flops 110592 | bytes 27712 | tf_op jit(solution)/shard_map/and | solution.py:98
  91.9 26.0 %all-to-all-done.1 = f32[16,1,24576]{2,1,0:T(1,128)S(1)} async-done(((f32[16,1,24576]{2,1,0:T(1,128)}), f32[16,1,24576]{2,1,0:T(1,128)S(1)}, u32[]{:S(2)}, u32[]{:S(2)}) %all-to-all-start.1) | async-done | bytes 1572896 | tf_op jit(solution)/shard_map/all_to_all | solution.py:87
  117.9 8.1 %gather_fusion = f32[3072,128]{1,0:T(8,128)S(1)} fusion(f32[3072,128]{1,0:T(8,128)S(1)} %bitcast.55, s32[3072]{0:T(1024)S(1)} %broadcast_clamp_fusion), kind=kCustom, calls=%fused_computation | custom fusion | bytes 3158016 | tf_op jit(solution)/shard_map/gather | solution.py:101
  126.0 2.5 %broadcast_select_fusion = f32[3072,128]{1,0:T(8,128)} fusion(f32[3072,128]{1,0:T(8,128)S(1)} %gather_fusion, pred[3072]{0:T(1024)(128)(4,1)S(1)} %get-tuple-element.5), kind=kLoop, calls=%fused_computation.23 | loop fusion | flops 393216 | bytes 3148800 | tf_op jit(solution)/shard_map/jit(_where)/select_n | solution.py:101
  (10 shorter events, 0.2 us)
Async XLA Ops:
  25.9 1.4 %copy-start = (f32[4096,128]{1,0:T(8,128)}, f32[4096,128]{1,0:T(8,128)S(1)}, u32[]{:S(2)}) copy-start(f32[4096,128]{1,0:T(8,128)S(1)} %slice.58) | copy-start | bytes 6291460
  27.3 1.6 %slice-start = ((f32[4096,144]{1,0:T(8,128)}), f32[4096,16]{1,0:T(8,128)S(1)}, s32[]{:S(2)}) async-start(f32[4096,144]{1,0:T(8,128)} %scatter_custom_fusion), calls=%async_computation.2 | async-start | bytes 4194304 | tf_op jit(solution)/shard_map/slice | solution.py:65
  27.3 20.7 %collective-permute-start = (f32[512,128]{1,0:T(8,128)S(1)}, f32[512,128]{1,0:T(8,128)S(1)}, u32[]{:S(2)}, u32[]{:S(2)}) collective-permute-start(f32[512,128]{1,0:T(8,128)S(1)} %constant_dynamic-slice_fusion), channel_id=1, source_target_pairs={{0,2},{2,4},{4,6},{6,8},{8,10},{10,12},{12,14},{14,16},{16,18},{18... | collective-permute-start | bytes 786440 | tf_op jit(solution)/shard_map/ppermute | solution.py:13
  33.2 40.4 %all-to-all-start = ((f32[16,1,1]{2,1,0:T(1,128)}), f32[16,1,1]{2,1,0:T(1,128)S(1)}, u32[]{:S(2)}, u32[]{:S(2)}) async-start(f32[16,1,1]{2,1,0:T(1,128)} %copy.33), calls=%async_computation | async-start | bytes 16384 | tf_op jit(solution)/shard_map/all_to_all | solution.py:88
  44.8 3.3 %copy-start.1 = (f32[4096,128]{1,0:T(8,128)S(1)}, f32[4096,128]{1,0:T(8,128)}, u32[]{:S(2)}) copy-start(f32[4096,128]{1,0:T(8,128)} %copy-done) | copy-start | bytes 6291460
  54.2 5.3 %copy-start.2 = (f32[128]{0:T(128)S(1)}, f32[128]{0:T(128)}, u32[]{:S(2)}) copy-start(f32[128]{0:T(128)} %param.7) | copy-start | bytes 1540
  73.6 44.3 %all-to-all-start.1 = ((f32[16,1,24576]{2,1,0:T(1,128)}), f32[16,1,24576]{2,1,0:T(1,128)S(1)}, u32[]{:S(2)}, u32[]{:S(2)}) async-start(f32[16,1,24576]{2,1,0:T(1,128)} %bitcast.29), calls=%async_computation.1 | async-start | bytes 3145728 | tf_op jit(solution)/shard_map/all_to_all | solution.py:87
where the time goes:
time: 129 us
  other arithmetic  44.6 us (35%)
  local copies, waits for them, and re-layouts  26.5 us (21%)
  waiting for transfers between devices  26 us (20%)
  starting transfers between devices  15.6 us (12%)
  matrix products  10.8 us (8%)
  blocking collectives  3.36 us (3%)
  between operations  1.56 us (1%)
    all_to_all x1, waiting for transfers between devices, local(): lax.all_to_all(outgoing, 'tm', split_axis=0, concat_axis=0, tiled=True)  26 us
    scatter x1, other arithmetic, compact_rows(): jnp.zeros((size_rows, width), jnp.float32).at[target]  20.2 us
    scatter x1, local copies, waits for them, and re-layouts, fill_slots(): jnp.zeros((slots_total, width), jnp.float32).at[slot]  12.1 us
    and x1, other arithmetic, local(): inside = (offset >= 0) & (offset < most)  9.94 us
    gather x1, local copies, waits for them, and re-layouts, local(): keyed = jnp.where(inside[:, None], flat[lookup], jnp.float32(0.0))  8.11 us
    all_to_all x1, starting transfers between devices, local(): lax.all_to_all(sideband, 'tm', split_axis=0, concat_axis=0, tiled=True)  7.17 us
    all_to_all x1, starting transfers between devices, local(): lax.all_to_all(outgoing, 'tm', split_axis=0, concat_axis=0, tiled=True)  6.92 us
    dot_general x1, matrix products, window_sums(): jnp.einsum('ij,bjf->bif', lower, blocks, precision=lax.Precision.HIGHEST)  3.91 us
  transfers between devices with their start and end apart: 3, of which 1 were waited for; matrix products, arithmetic and copies ran while one was open for 35% of the time, Pallas kernels for 0%

commit v1 on v0

--- a/solution.py
+++ b/solution.py
@@ -76,7 +76,7 @@
     extended = jnp.concatenate([earlier_tail, compact], axis=0)
     sums = window_sums(extended, WINDOW)
     squares = jnp.sum(sums * sums, axis=1)
-    full = lax.psum(squares, "rep")
+    full = jnp.sum(lax.all_gather(squares, "rep"), axis=0)
     values = sums * gain[None, :] / jnp.sqrt(full[:, None] / F + epsilon)
     local_rank, counts = bucket_ranks(hits)
     slot = jnp.where(valid, compact_key * most + local_rank, nodes * most)

time: 129 us -> 128 us (level)
  blocking collectives: 3.36 us -> 1.83 us
    psum x1 -> x0, blocking collectives: 3.36 us -> none  [local(): full = lax.psum(squares, 'rep')]
    all_gather x0 -> x1, blocking collectives: none -> 1.83 us  [local(): full = jnp.sum(lax.all_gather(squares, 'rep'), axis=0)]
  transfers between devices with their start and end apart: 3 -> 3, of which waited for: 1 -> 1; matrix products, arithmetic and copies ran while one was open for 35% -> 36% of each run, Pallas kernels for 0% -> 0%
where the time goes in v1:
time: 128 us; the launch traced here: 127 us
  other arithmetic  44.7 us (35%)
  local copies, waits for them, and re-layouts  26.5 us (21%)
  waiting for transfers between devices  25.9 us (20%)
  starting transfers between devices  15.6 us (12%)
  matrix products  10.8 us (8%)
  blocking collectives  1.83 us (1%)
  between operations  1.57 us (1%)
    all_to_all x1, waiting for transfers between devices, local(): lax.all_to_all(outgoing, 'tm', split_axis=0, concat_axis=0, tiled=True)  25.9 us
    scatter x1, other arithmetic, compact_rows(): jnp.zeros((size_rows, width), jnp.float32).at[target]  20.2 us
    scatter x1, local copies, waits for them, and re-layouts, fill_slots(): jnp.zeros((slots_total, width), jnp.float32).at[slot]  12.1 us
    and x1, other arithmetic, local(): inside = (offset >= 0) & (offset < most)  9.94 us
    gather x1, local copies, waits for them, and re-layouts, local(): keyed = jnp.where(inside[:, None], flat[lookup], jnp.float32(0.0))  8.11 us
    all_to_all x1, starting transfers between devices, local(): lax.all_to_all(sideband, 'tm', split_axis=0, concat_axis=0, tiled=True)  7.17 us
    all_to_all x1, starting transfers between devices, local(): lax.all_to_all(outgoing, 'tm', split_axis=0, concat_axis=0, tiled=True)  6.92 us
    dot_general x1, matrix products, window_sums(): jnp.einsum('ij,bjf->bif', lower, blocks, precision=lax.Precision.HIGHEST)  3.91 us
  transfers between devices with their start and end apart: 3, of which 1 were waited for; matrix products, arithmetic and copies ran while one was open for 36% of the time, Pallas kernels for 0%

profile of v1, /device:TPU:12, one launch (start us, length us, event | category | flops | bytes accessed | tf_op | source)
XLA Modules:
  0.0 127.0 jit_solution(14809261609317191149)
XLA Ops:
  0.0 1.0 reduce-window.14
  1.0 0.1 slice.54
  1.1 0.1 reduce-window.18
  1.1 0.1 slice_reduce_fusion.2
  1.2 1.4 %fusion.20 = (s32[]{:T(128)}, s32[4096]{0:T(1024)S(1)}) fusion(s32[4096]{0:T(1024)} %param.5, s32[32,128]{1,0:T(8,128)S(1)} %reduce-window.14, s32[32]{0:T(128)S(1)} %slice_reduce_fusion.2), kind=kLoop, calls=%fused_computation.53 | loop fusion | flops 32767 | bytes 49284 | tf_op jit(solution)/shard_map/reduce_sum | solution.py:60
  2.7 1.3 %fusion.7 = f32[4096,16]{1,0:T(8,128)S(1)} fusion(s32[4096]{0:T(1024)} %param.6), kind=kLoop, calls=%fused_computation.17 | loop fusion | flops 131072 | bytes 278528 | tf_op jit(solution)/shard_map/convert_element_type | solution.py:61
  4.0 20.2 %scatter_custom_fusion = f32[4096,144]{1,0:T(8,128)} fusion(s32[4096]{0:T(1024)S(1)} %get-tuple-element.10, f32[4096,16]{1,0:T(8,128)S(1)} %fusion.7, f32[]{:T(128)} %constant.74, f32[4096,128]{1,0:T(8,128)} %param.4, f32[]{:T(128)} %constant.14.clone.1), kind=kCustom, calls=%fused_computation.3 | custom fusion | flops 589824 | bytes 6553608 | tf_op jit(solution)/shard_map/scatter | solution.py:46
  24.2 1.7 %slice.58 = f32[4096,128]{1,0:T(8,128)S(1)} slice(f32[4096,144]{1,0:T(8,128)} %scatter_custom_fusion), slice={[0:4096], [0:128]} | slice | bytes 4194304 | tf_op jit(solution)/shard_map/slice | solution.py:64
  25.9 0.0 copy-start
  27.3 0.0 copy-done
  27.3 0.0 slice-start
  27.3 1.5 %collective-permute-start = (f32[512,128]{1,0:T(8,128)S(1)}, f32[512,128]{1,0:T(8,128)S(1)}, u32[]{:S(2)}, u32[]{:S(2)}) collective-permute-start(f32[512,128]{1,0:T(8,128)S(1)} %constant_dynamic-slice_fusion), channel_id=1, source_target_pairs={{0,2},{2,4},{4,6},{6,8},{8,10},{10,12},{12,14},{14,16},{16,18},{18... | collective-permute-start | bytes 786440 | tf_op jit(solution)/shard_map/ppermute | solution.py:13
  28.9 0.0 slice-done
  28.9 3.4 %convolution_bitcast_fusion.1 = f32[8,512,16]{1,2,0:T(8,128)S(1)} fusion(f32[8,512,16]{2,1,0:T(8,128)S(1)} %bitcast.54), kind=kOutput, calls=%fused_computation.19 | convolution fusion | flops 402915328 | bytes 524288 | tf_op jit(solution)/shard_map/ij,bjc->bic/dot_general | solution.py:32
  32.3 0.2 slice_reduce_fusion.1
  32.5 0.7 copy.33
  33.2 7.2 %all-to-all-start = ((f32[16,1,1]{2,1,0:T(1,128)}), f32[16,1,1]{2,1,0:T(1,128)S(1)}, u32[]{:S(2)}, u32[]{:S(2)}) async-start(f32[16,1,1]{2,1,0:T(1,128)} %copy.33), calls=%async_computation | async-start | bytes 16384 | tf_op jit(solution)/shard_map/all_to_all | solution.py:88
  40.4 0.2 fusion.22
  40.5 3.5 %fusion.15 = f32[1,4096]{1,0:T(1,128)S(1)} fusion(f32[4096,144]{1,0:T(8,128)} %scatter_custom_fusion), kind=kOutput, calls=%fused_computation.45 | convolution fusion | flops 786448 | bytes 2113536 | tf_op jit(solution)/shard_map/dot_general | solution.py:67
  44.0 0.1 broadcast_add_fusion
  44.1 0.6 copy.43
  44.8 0.0 copy-start.1
  44.8 2.6 %fusion.5 = f32[4096]{0:T(1024)S(1)} fusion(f32[8,512,16]{2,1,0:T(8,128)S(1)} %copy.43, f32[4096,144]{1,0:T(8,128)} %scatter_custom_fusion), kind=kLoop, calls=%fused_computation.13 | loop fusion | flops 126976 | bytes 540672 | tf_op jit(solution)/shard_map/reduce_sum | solution.py:36
  47.3 0.7 compare_select_fusion.1
  48.0 0.0 collective-permute-done
  48.0 0.0 copy-done.1
  48.0 0.2 pad_maximum_fusion
  48.2 3.9 %convolution_bitcast_fusion = f32[9,512,128]{1,2,0:T(8,128)S(1)} fusion(f32[9,512,128]{2,1,0:T(8,128)S(1)} %bitcast.55), kind=kOutput, calls=%fused_computation.18 | convolution fusion | flops 3624140800 | bytes 4718592 | tf_op jit(solution)/shard_map/ij,bjf->bif/dot_general | solution.py:20
  52.1 0.4 slice_reduce_fusion
  52.5 1.8 %multiply_reduce_fusion = (f32[8,512]{1,0:T(8,128)S(1)}, f32[8,512,128]{1,2,0:T(8,128)}) fusion(f32[9,512,128]{1,2,0:T(8,128)S(1)} %convolution_bitcast_fusion, f32[8,128]{1,0:T(8,128)S(1)} %slice_reduce_fusion), kind=kLoop, calls=%fused_computation.14 | loop fusion | flops 2093056 | bytes 6311936 | tf_op jit(solution)/shard_map/reduce_sum | solution.py:78
  54.2 0.0 copy-start.2
  54.2 1.9 %copy.38 = f32[8,512,128]{2,1,0:T(8,128)S(1)} copy(f32[8,512,128]{1,2,0:T(8,128)} %get-tuple-element.8) | data formatting | bytes 4194304 | tf_op jit(solution)/shard_map/sub | solution.py:22
  56.2 1.8 %all-gather = f32[2,1,4096]{2,1,0:T(1,128)S(1)} all-gather(f32[1,1,4096]{2,1,0:T(1,128)S(1)} %reshape.220), channel_id=1, replica_groups=mesh['tm'=16,'rep'=2] {'rep'}, dimensions={0}, use_global_device_ids=true | all-gather | bytes 49152 | tf_op jit(solution)/shard_map/all_gather | solution.py:79
  58.1 0.0 copy-done.2
  58.1 1.9 %fusion.4 = f32[4096,128]{1,0:T(8,128)} fusion(f32[8,512,128]{2,1,0:T(8,128)S(1)} %copy.38, f32[4096]{0:T(1024)S(1)} %add_sqrt_fusion, f32[128]{0:T(128)S(1)} %copy-done.2), kind=kLoop, calls=%fused_computation.11 | loop fusion | flops 1048576 | bytes 4211200 | tf_op jit(solution)/shard_map/div | solution.py:80
  60.0 12.1 %scatter_custom_fusion.1 = f32[3072,128]{1,0:T(8,128)} fusion(s32[4096]{0:T(1024)S(1)} %compare_select_fusion.1, f32[4096,128]{1,0:T(8,128)} %fusion.4, f32[]{:T(128)} %constant.14.clone.1), kind=kCustom, calls=%fused_computation.24 | custom fusion | bytes 1573376 | tf_op jit(solution)/shard_map/scatter | solution.py:51
  72.1 0.0 all-to-all-done
  72.1 6.9 %all-to-all-start.1 = ((f32[16,1,24576]{2,1,0:T(1,128)}), f32[16,1,24576]{2,1,0:T(1,128)S(1)}, u32[]{:S(2)}, u32[]{:S(2)}) async-start(f32[16,1,24576]{2,1,0:T(1,128)} %bitcast.29), calls=%async_computation.1 | async-start | bytes 3145728 | tf_op jit(solution)/shard_map/all_to_all | solution.py:87
  79.1 0.1 reduce.4
  79.2 0.4 convert_reduce_fusion.1
  79.6 0.7 fusion.21
  80.3 0.1 convert_reduce_fusion
  80.5 9.9 %compare_and_fusion = (pred[3072]{0:T(1024)(128)(4,1)S(1)}, s32[3072]{0:T(1024)S(1)}) fusion(s32[]{:T(128)} %bitcast.22, s32[]{:T(128)} %bitcast.21, s32[]{:T(128)} %bitcast.20, s32[]{:T(128)} %bitcast.19, s32[]{:T(128)} %bitcast.18, s32[]{:T(128)} %bitcast.17, s32[]{:T(128)} %bitcast.16, s32[]{:T(128)} %bitcast.15, s32[]{:T(128)} %bitcast.14, s32[]{:T(128)} %bitcast.13, ...), kind=kLoop, calls=%fused_computation.42 | loop fusion | flops 110592 | bytes 27712 | tf_op jit(solution)/shard_map/and | solution.py:98
  90.5 25.9 %all-to-all-done.1 = f32[16,1,24576]{2,1,0:T(1,128)S(1)} async-done(((f32[16,1,24576]{2,1,0:T(1,128)}), f32[16,1,24576]{2,1,0:T(1,128)S(1)}, u32[]{:S(2)}, u32[]{:S(2)}) %all-to-all-start.1) | async-done | bytes 1572896 | tf_op jit(solution)/shard_map/all_to_all | solution.py:87
  116.4 8.1 %gather_fusion = f32[3072,128]{1,0:T(8,128)S(1)} fusion(f32[3072,128]{1,0:T(8,128)S(1)} %bitcast.53, s32[3072]{0:T(1024)S(1)} %broadcast_clamp_fusion), kind=kCustom, calls=%fused_computation | custom fusion | bytes 3158016 | tf_op jit(solution)/shard_map/gather | solution.py:101
  124.5 2.5 %broadcast_select_fusion = f32[3072,128]{1,0:T(8,128)} fusion(f32[3072,128]{1,0:T(8,128)S(1)} %gather_fusion, pred[3072]{0:T(1024)(128)(4,1)S(1)} %get-tuple-element.5), kind=kLoop, calls=%fused_computation.23 | loop fusion | flops 393216 | bytes 3148800 | tf_op jit(solution)/shard_map/jit(_where)/select_n | solution.py:101
  (11 shorter events, 0.2 us)
Async XLA Ops:
  25.9 1.4 %copy-start = (f32[4096,128]{1,0:T(8,128)}, f32[4096,128]{1,0:T(8,128)S(1)}, u32[]{:S(2)}) copy-start(f32[4096,128]{1,0:T(8,128)S(1)} %slice.58) | copy-start | bytes 6291460
  27.3 1.6 %slice-start = ((f32[4096,144]{1,0:T(8,128)}), f32[4096,16]{1,0:T(8,128)S(1)}, s32[]{:S(2)}) async-start(f32[4096,144]{1,0:T(8,128)} %scatter_custom_fusion), calls=%async_computation.2 | async-start | bytes 4194304 | tf_op jit(solution)/shard_map/slice | solution.py:65
  27.3 20.7 %collective-permute-start = (f32[512,128]{1,0:T(8,128)S(1)}, f32[512,128]{1,0:T(8,128)S(1)}, u32[]{:S(2)}, u32[]{:S(2)}) collective-permute-start(f32[512,128]{1,0:T(8,128)S(1)} %constant_dynamic-slice_fusion), channel_id=1, source_target_pairs={{0,2},{2,4},{4,6},{6,8},{8,10},{10,12},{12,14},{14,16},{16,18},{18... | collective-permute-start | bytes 786440 | tf_op jit(solution)/shard_map/ppermute | solution.py:13
  33.2 38.9 %all-to-all-start = ((f32[16,1,1]{2,1,0:T(1,128)}), f32[16,1,1]{2,1,0:T(1,128)S(1)}, u32[]{:S(2)}, u32[]{:S(2)}) async-start(f32[16,1,1]{2,1,0:T(1,128)} %copy.33), calls=%async_computation | async-start | bytes 16384 | tf_op jit(solution)/shard_map/all_to_all | solution.py:88
  44.8 3.3 %copy-start.1 = (f32[4096,128]{1,0:T(8,128)S(1)}, f32[4096,128]{1,0:T(8,128)}, u32[]{:S(2)}) copy-start(f32[4096,128]{1,0:T(8,128)} %copy-done) | copy-start | bytes 6291460
  54.2 3.9 %copy-start.2 = (f32[128]{0:T(128)S(1)}, f32[128]{0:T(128)}, u32[]{:S(2)}) copy-start(f32[128]{0:T(128)} %param.7) | copy-start | bytes 1540
  72.1 44.2 %all-to-all-start.1 = ((f32[16,1,24576]{2,1,0:T(1,128)}), f32[16,1,24576]{2,1,0:T(1,128)S(1)}, u32[]{:S(2)}, u32[]{:S(2)}) async-start(f32[16,1,24576]{2,1,0:T(1,128)} %bitcast.29), calls=%async_computation.1 | async-start | bytes 3145728 | tf_op jit(solution)/shard_map/all_to_all | solution.py:87
